TPU v7x, 32 devices: a whole 2x2x4 slice. The times are simulated.
32 devices in a mesh: dp: 16 (over z, y, x), mp: 2 (over core).
Axes of the slice: x: 2, y: 2, z: 4, core: 2. Of those that a mesh axis runs over, the one named last changes fastest.
Arguments:
- points: bfloat16 [16384, 1024], P(('dp', 'mp')), may hold values from -6 to 6
- centroids: bfloat16 [4096, 1024], P('mp'), may hold values from -6 to 6
- assign: int32 [16384], P(('dp', 'mp')), may hold values from 0 to 4095
- keep_mask: int32 [16384], P(('dp', 'mp')), may hold values 0 or 1
Outputs:
- new_centroids: float32 [4096, 1024], P('mp')
- row_cost: float32 [16384], P(('dp', 'mp'))
All inputs are finite; a program needn't handle non-finite values. No bound on the sum of `keep_mask` on one device may be relied on, other than what follows from the above.
Results may differ from a plain program's by a relative error of at most 0.0008.
Values may be sent and summed in bfloat16 or wider, within the bound.
A program may use at most 128 MiB of HBM per device.

v0:
```python
import jax
import jax.numpy as jnp
from jax import lax
from jax.sharding import PartitionSpec as P


def update(sums, counts, prior):
    fresh = sums / jnp.maximum(counts, 1.0)[:, None]
    return jnp.where(counts[:, None] > 0.5, fresh, prior)


def shards(points, centroids, assign, keep_mask):
    width = points.shape[1]
    point_f = points.astype(jnp.float32)
    point_sq = jnp.sum(point_f * point_f, axis=1)
    piece = lax.all_gather(centroids, "mp", axis=0, tiled=True)
    inner = lax.dot_general(
        points, piece, (((1,), (1,)), ((), ())), preferred_element_type=jnp.float32
    )
    piece_f = piece.astype(jnp.float32)
    cent_sq = jnp.sum(piece_f * piece_f, axis=1)
    dist = point_sq[:, None] - 2.0 * inner + cent_sq[None, :]
    row_cost = jnp.min(dist, axis=1) / width
    shard_rows = centroids.shape[0]
    mp_count = lax.axis_size("mp")
    dp_count = lax.axis_size("dp")
    total = shard_rows * mp_count
    weights = keep_mask.astype(jnp.float32)
    block_rows = shard_rows // dp_count
    owner = assign // shard_rows
    within = assign % shard_rows
    target = (
        within // block_rows * (mp_count * block_rows) + owner * block_rows + within % block_rows
    )
    onehot = (jnp.arange(total, dtype=jnp.int32)[:, None] == target[None, :]).astype(
        jnp.float32
    ) * weights[None, :]
    counts = jnp.sum(onehot, axis=1)
    sums = jnp.dot(onehot.astype(jnp.bfloat16), points, preferred_element_type=jnp.float32)
    part_sums, part_counts = (
        lax.psum_scatter(sums, ("dp", "mp"), scatter_dimension=0, tiled=True),
        lax.psum_scatter(counts, ("dp", "mp"), scatter_dimension=0, tiled=True),
    )
    prior = lax.dynamic_slice_in_dim(
        centroids, lax.axis_index("dp") * block_rows, block_rows, 0
    ).astype(jnp.float32)
    fresh = update(part_sums, part_counts, prior)
    new_centroids = lax.all_gather(fresh, "dp", axis=0, tiled=True)
    return (new_centroids, row_cost)


def solution(mesh):
    in_specs = (P(("dp", "mp"), None), P("mp", None), P(("dp", "mp")), P(("dp", "mp")))
    out_specs = (P("mp", None), P(("dp", "mp")))
    return jax.shard_map(shards, mesh=mesh, in_specs=in_specs, out_specs=out_specs, check_vma=False)
```

profile of v0, /device:TPU:0, one launch (start us, length us, event | category | flops | bytes accessed | tf_op | source)
XLA Modules:
  0.0 338.7 jit_solution(8034875120755660184)
XLA Ops:
  8.0 0.0 reduce-scatter.2.cloned.1.call-start
  8.0 0.7 convert_element_type.16
  8.7 0.7 fusion.6
  9.4 9.3 %fusion = f32[4096,1024]{1,0:T(8,128)} fusion(bf16[512,1024]{1,0:T(8,128)(2,1)} %param.4, f32[512]{0:T(512)S(1)} %convert_element_type.16, s32[512]{0:T(512)S(1)} %fusion.6), kind=kOutput, calls=%fused_computation.5 | convolution fusion | flops 4299161600 | bytes 17829888 | tf_op jit(solution)/shard_map/dot_general | solution.py:39
  18.7 0.0 copy-start.1
  18.7 0.0 reduce-scatter.2.cloned.1.call-update
  18.8 0.0 all-gather.5.cloned.1.call-start
  18.8 0.5 all-gather.5.cloned.1.call-update
  19.3 0.0 all-gather.3.cloned.1.call-start
  19.4 1.0 select_reduce_fusion
  20.4 48.9 %all-reduce = f32[4096]{0:T(1024)S(1)} all-reduce(f32[4096]{0:T(1024)S(1)} %select_reduce_fusion), channel_id=2, replica_groups=mesh['dp'=16,'mp'=2] {'dp','mp'}, use_global_device_ids=true, to_apply=%region_1.0.clone | all-reduce | flops 4096 | bytes 32768
  69.3 0.1 broadcast_compare_fusion
  69.3 0.1 broadcast_maximum_fusion
  69.4 137.0 %reduce-scatter.2.cloned.1.call-done = f32[128,1024]{1,0:T(8,128)} async-done(((f32[4096,1024]{1,0:T(8,128)}), f32[128,1024]{1,0:T(8,128)}) %reduce-scatter.2.cloned.1.call-update) | async-done | bytes 524304 | tf_op jit(solution)/shard_map/reduce_scatter | solution.py:41
  206.4 2.0 convert_select_fusion
  208.4 0.0 all-gather.3.cloned.1.call-update
  208.4 0.0 copy-done.1
  208.4 0.3 multiply_reduce_fusion.1
  208.7 0.0 all-gather.5.cloned.1.call-done
  208.7 0.0 copy-start
  208.8 5.2 %multiply_reduce_fusion = f32[4096]{0:T(1024)S(1)} fusion(bf16[4096,1024]{1,0:T(8,128)(2,1)} %all-gather.5.cloned.1.call-done), kind=kLoop, calls=%fused_computation | loop fusion | flops 12578816 | bytes 8404992 | tf_op jit(solution)/shard_map/reduce_sum | solution.py:21
  214.0 0.5 copy-done
  214.5 5.1 %add_reduce_fusion = f32[512]{0:T(512)S(1)} fusion(bf16[512,1024]{1,0:T(8,128)(2,1)S(1)} %copy-done.1, bf16[4096,1024]{1,0:T(8,128)(2,1)S(1)} %copy-done, f32[4096]{0:T(1024)S(1)} %multiply_reduce_fusion, f32[512]{0:T(512)S(1)} %multiply_reduce_fusion.1), kind=kOutput, calls=%fused_computation.3 | convolution fusion | flops 4303355392 | bytes 9457664 | tf_op jit(solution)/shard_map/dot_general | solution.py:17
  219.6 0.6 broadcast_multiply_fusion
  220.2 102.7 %all-gather.3.cloned.1.call-done = f32[2048,1024]{1,0:T(8,128)} async-done(((f32[128,1024]{1,0:T(8,128)}), f32[2048,1024]{1,0:T(8,128)}) %all-gather.3.cloned.1.call-update) | async-done | bytes 8388624 | tf_op jit(solution)/shard_map/all_gather | solution.py:48
  322.8 8.4 %copy.7 = f32[2048,1024]{1,0:T(8,128)} copy(f32[2048,1024]{1,0:T(8,128)} %all-gather.3.cloned.1.call-done) | data formatting | bytes 16777216
Async XLA Ops:
  8.0 198.4 %reduce-scatter.2.cloned.1.call-start = ((), (), s32[]{:S(2)}) async-start(), calls=%async_computation.1 | async-start | bytes 17301504 | tf_op jit(solution)/shard_map/reduce_scatter | solution.py:41
  18.7 189.7 %copy-start.1 = (bf16[512,1024]{1,0:T(8,128)(2,1)S(1)}, bf16[512,1024]{1,0:T(8,128)(2,1)}, u32[]{:S(2)}) copy-start(bf16[512,1024]{1,0:T(8,128)(2,1)} %param.4) | copy-start | bytes 3145732
  18.8 190.0 %all-gather.5.cloned.1.call-start = ((), (), s32[]{:S(2)}) async-start(), calls=%async_computation.3 | async-start | bytes 12582912 | tf_op jit(solution)/shard_map/all_gather | solution.py:16
  19.3 303.5 %all-gather.3.cloned.1.call-start = ((), (), s32[]{:S(2)}) async-start(), calls=%async_computation.2 | async-start | bytes 8912896 | tf_op jit(solution)/shard_map/all_gather | solution.py:48
  208.7 5.8 %copy-start = (bf16[4096,1024]{1,0:T(8,128)(2,1)S(1)}, bf16[4096,1024]{1,0:T(8,128)(2,1)}, u32[]{:S(2)}) copy-start(bf16[4096,1024]{1,0:T(8,128)(2,1)} %all-gather.5.cloned.1.call-done) | copy-start | bytes 25165828
Sparse Core Ops, SparseCore 0:
  18.9 187.4 reduce-scatter.1
Sparse Core Ops, SparseCore 1:
  20.8 22.4 all-gather.4
  208.5 114.3 all-gather.2
where the time goes:
time: 339 us
  waiting for transfers between devices  240 us (71%)
  blocking collectives  48.9 us (14%)
  between operations  15.5 us (5%)
  matrix products  14.4 us (4%)
  other arithmetic  10.6 us (3%)
  local copies, waits for them, and re-layouts  8.96 us (3%)
    reduce_scatter x1, waiting for transfers between devices, shards(): lax.psum_scatter(sums, ('dp', 'mp'), scatter_dimension=0, tiled=True)  137 us
    all_gather x1, waiting for transfers between devices, shards(): new_centroids = lax.all_gather(fresh, 'dp', axis=0, tiled=True)  103 us
    unnamed x1, blocking collectives  48.9 us
    dot_general x1, matrix products, shards(): jnp.dot(onehot.astype(jnp.bfloat16), points, preferred_element_type=jnp.f...  9.3 us
    unnamed x5, local copies, waits for them, and re-layouts  8.96 us
  transfers between devices with their start and end apart: 3, of which 2 were waited for; matrix products, arithmetic and copies ran while one was open for 4% of the time, Pallas kernels for 0%

commit v1 on v0

v1 whole, which is shorter than its diff:
```python
import functools

import jax
import jax.numpy as jnp
from jax import lax
from jax.experimental import pallas as pl
from jax.experimental.pallas import tpu as pltpu
from jax.sharding import Mesh
from jax.sharding import PartitionSpec as P

STEPS = 32000.0
TINY = 2.0**-100
EXTRA = 8
PLANE = 4
LANES = 128


def remote(src, dst, send, recv, device):
    return pltpu.make_async_remote_copy(
        src_ref=src,
        dst_ref=dst,
        send_sem=send,
        recv_sem=recv,
        device_id=device,
        device_id_type=pl.DeviceIdType.MESH,
    )


def greet(peers):
    barrier = pltpu.get_barrier_semaphore()
    for peer in peers:
        pl.semaphore_signal(barrier, inc=1, device_id=peer, device_id_type=pl.DeviceIdType.MESH)
    pl.semaphore_wait(barrier, len(peers))


def update_kernel(
    z_n, shard_rows, p_ref, id_ref, prior_ref, out_ref,
    near, idn, acc, mrecv, red, zrecv,
    ps, pr, ids_s, ids_r, ms, mr, zs, zr, gs, gr, xs, xr, ys, yr, ds_, dr,
):
    z, q, m = lax.axis_index("z"), lax.axis_index("q"), lax.axis_index("mp")
    nx = q + 1 - 2 * lax.rem(q, 2)
    ny = lax.rem(q + 2, PLANE)
    nd = ny + 1 - 2 * lax.rem(ny, 2)
    other = 1 - m
    rows, width = p_ref.shape
    block = prior_ref.shape[0]
    half = rows // 2
    peers = [(z, nx, m), (z, ny, m), (z, nd, m), (z, q, other)]
    greet(peers + [(lax.rem(z + d, z_n), q, m) for d in range(1, z_n)])

    id_copies = [
        remote(id_ref, idn.at[k], ids_s.at[k], ids_r.at[k], (z, to, m))
        for k, to in enumerate((nx, ny, nd))
    ]
    for c in id_copies:
        c.start()
    lo, hi = pl.ds(0, half), pl.ds(half, half)

    def piece(k, src, slot, part, to):
        return remote(src, near.at[slot, part], ps.at[k], pr.at[k], (z, to, m))

    a = piece(0, p_ref.at[lo], 0, lo, nx)
    c = piece(1, p_ref.at[hi], 1, hi, ny)
    b = piece(2, p_ref.at[hi], 0, hi, nx)
    d_ = piece(3, p_ref.at[lo], 1, lo, ny)
    e = piece(4, near.at[0, lo], 2, lo, ny)
    f = piece(5, near.at[1, hi], 2, hi, nx)
    for copy in (a, c, b, d_):
        copy.start()

    def add(ids, pts, first):
        def tile(t, carry):
            base = (t // z_n) * shard_rows + (lax.rem(t, z_n) * PLANE + q) * block
            row = base + lax.broadcasted_iota(jnp.int32, (block, rows), 0)
            hit = jnp.where(row == ids[0:1, :], 1.0, 0.0)
            part = jnp.dot(hit.astype(jnp.bfloat16), pts[...], preferred_element_type=jnp.float32)
            count = jnp.broadcast_to(jnp.sum(hit, axis=1, keepdims=True), (block, LANES))
            if first:
                acc[t, :, :width] = part
                acc[t, :, width:] = count
            else:
                acc[t, :, :width] += part
                acc[t, :, width:] += count
            return carry

        lax.fori_loop(0, 2 * z_n, tile, 0)

    add(id_ref, p_ref, True)
    a.wait_recv()
    e.start()
    c.wait_recv()
    f.start()
    for copy in id_copies:
        copy.wait_recv()
    b.wait_recv()
    add(idn.at[0], near.at[0], False)
    d_.wait_recv()
    add(idn.at[1], near.at[1], False)
    e.wait_recv()
    f.wait_recv()
    add(idn.at[2], near.at[2], False)

    mcopy = remote(acc.at[pl.ds(other * z_n, z_n)], mrecv, ms, mr, (z, q, other))
    mcopy.start()
    mcopy.wait_recv()

    zcopies = []
    for k in range(1, z_n + 1):
        to = lax.rem(z + k, z_n)
        red[to] = acc[m * z_n + to] + mrecv[to]
        if k < z_n:
            copy = remote(red.at[to], zrecv.at[k - 1], zs.at[k - 1], zr.at[k - 1], (to, q, m))
            copy.start()
            zcopies.append(copy)
    for k in range(1, z_n):
        zcopies[k - 1].wait_recv()
        red[z] += zrecv[k - 1]

    sums = red[z, :, :width]
    count = red[z, :, width : width + 1]
    fresh = jnp.where(
        count > 0.5, sums / jnp.maximum(count, 1.0), prior_ref[...].astype(jnp.float32)
    )
    own = z * PLANE + q
    half_w = width // 2
    top = jnp.max(jnp.abs(fresh), axis=1, keepdims=True)
    power = jnp.ceil(jnp.log2(jnp.maximum(top, TINY)))
    code = jnp.floor(fresh * jnp.exp2(-power) * STEPS + 0.5).astype(jnp.int32)
    out_ref[own, :block] = (code[:, :half_w] << 16) | (code[:, half_w:] & 0xFFFF)
    at_row = lax.broadcasted_iota(jnp.int32, (block, LANES), 0)
    at_lane = lax.broadcasted_iota(jnp.int32, (block, LANES), 1)
    flat = jnp.sum(jnp.where(at_row == at_lane, power, 0.0), axis=0, keepdims=True)
    out_ref[own, block:] = jnp.zeros((EXTRA, half_w), jnp.int32)
    out_ref[own, block:, :LANES] = jnp.broadcast_to(flat.astype(jnp.int32), (EXTRA, LANES))

    def pass_on(index, send, recv, device):
        copy = remote(out_ref.at[index], out_ref.at[index], send, recv, device)
        copy.start()
        return copy

    gcopies = [
        pass_on(own, gs.at[k - 1], gr.at[k - 1], (lax.rem(z + k, z_n), q, m))
        for k in range(1, z_n)
    ]
    xc, yc, dc = [], [], []

    def relay(k):
        base = lax.rem(z + z_n - k, z_n) * PLANE
        if k % 2 == 0:
            xc[k].wait_recv()
            dc.append(pass_on(base + nx, ds_.at[k], dr.at[k], (z, ny, m)))
        else:
            yc[k].wait_recv()
            dc.append(pass_on(base + ny, ds_.at[k], dr.at[k], (z, nx, m)))

    for k in range(z_n):
        mine = lax.rem(z + z_n - k, z_n) * PLANE + q
        if k > 0:
            gcopies[k - 1].wait_recv()
        xc.append(pass_on(mine, xs.at[k], xr.at[k], (z, nx, m)))
        yc.append(pass_on(mine, ys.at[k], yr.at[k], (z, ny, m)))
        if k > 0:
            relay(k - 1)
    relay(z_n - 1)
    for k in range(z_n):
        if k % 2 == 0:
            yc[k].wait_recv()
        else:
            xc[k].wait_recv()
        dc[k].wait_recv()
    for copy in id_copies + [a, b, c, d_, e, f, mcopy] + zcopies + gcopies + xc + yc + dc:
        copy.wait_send()


def shards(points, centroids, assign, keep_mask):
    rows, width = points.shape
    shard_rows = centroids.shape[0]
    z_n = lax.axis_size("z")
    dp_n = z_n * PLANE
    block = shard_rows // dp_n
    own = lax.axis_index("z") * PLANE + lax.axis_index("q")
    ids = jnp.where(keep_mask > 0, assign, -1)
    ids = jnp.broadcast_to(ids[None, :], (8, rows))
    prior = lax.dynamic_slice_in_dim(centroids, own * block, block, 0)
    vmem = pl.BlockSpec(memory_space=pltpu.VMEM)
    dma = pltpu.SemaphoreType.DMA
    wide = width + LANES
    back = pl.pallas_call(
        functools.partial(update_kernel, z_n, shard_rows),
        out_shape=jax.ShapeDtypeStruct((dp_n, block + EXTRA, width // 2), jnp.int32),
        in_specs=[vmem] * 3,
        out_specs=vmem,
        scratch_shapes=[
            pltpu.VMEM((3, rows, width), points.dtype),
            pltpu.VMEM((3, 8, rows), jnp.int32),
            pltpu.VMEM((2 * z_n, block, wide), jnp.float32),
            pltpu.VMEM((z_n, block, wide), jnp.float32),
            pltpu.VMEM((z_n, block, wide), jnp.float32),
            pltpu.VMEM((z_n - 1, block, wide), jnp.float32),
            dma((6,)), dma((6,)), dma((3,)), dma((3,)), dma, dma,
            dma((z_n - 1,)), dma((z_n - 1,)), dma((z_n - 1,)), dma((z_n - 1,)),
            dma((z_n,)), dma((z_n,)), dma((z_n,)), dma((z_n,)), dma((z_n,)), dma((z_n,)),
        ],
        compiler_params=pltpu.CompilerParams(
            collective_id=0, has_side_effects=True, vmem_limit_bytes=48 * 1024 * 1024
        ),
        cost_estimate=pl.CostEstimate(
            flops=0, bytes_accessed=200 * 1024 * 1024, transcendentals=0
        ),
    )(points, ids, prior)
    codes = back[:, :block]
    powers = back[:, block, :block].astype(jnp.float32)
    scale = (jnp.exp2(powers) / STEPS)[:, :, None]
    pair = jnp.concatenate([codes >> 16, (codes << 16) >> 16], axis=2)
    new_centroids = (pair.astype(jnp.float32) * scale).reshape(shard_rows, width)

    piece = lax.all_gather(centroids, "mp", axis=0, tiled=True)
    inner = lax.dot_general(
        points, piece, (((1,), (1,)), ((), ())), preferred_element_type=jnp.float32
    )
    point_f = points.astype(jnp.float32)
    point_sq = jnp.sum(point_f * point_f, axis=1)
    piece_f = piece.astype(jnp.float32)
    cent_sq = jnp.sum(piece_f * piece_f, axis=1)
    dist = point_sq[:, None] - 2.0 * inner + cent_sq[None, :]
    row_cost = jnp.min(dist, axis=1) / width
    return new_centroids, row_cost


def solution(mesh):
    dp, mp = mesh.shape["dp"], mesh.shape["mp"]
    grid = Mesh(mesh.devices.reshape(dp // PLANE, PLANE, mp), ("z", "q", "mp"))
    rows = ("z", "q", "mp")
    in_specs = (P(rows, None), P("mp", None), P(rows), P(rows))
    out_specs = (P("mp", None), P(rows))
    return jax.shard_map(shards, mesh=grid, in_specs=in_specs, out_specs=out_specs, check_vma=False)
```

time: 339 us -> 193 us (0.57)
  waiting for transfers between devices: 240 us -> 0.68 us
  Pallas kernels: 0 us -> 156 us
  blocking collectives: 48.9 us -> 0 us
  local copies, waits for them, and re-layouts: 8.96 us -> 2.2 us
  matrix products: 14.4 us -> 8.53 us
    pallas_call x0 -> x1, Pallas kernels: none -> 156 us  [shards(): pl.pallas_call(functools.partial(update_kernel, z_n, shard_rows), out_sha...]
    reduce_scatter x1 -> x0, waiting for transfers between devices: 137 us -> none  [shards(): lax.psum_scatter(sums, ('dp', 'mp'), scatter_dimension=0, tiled=True)]
    all_gather x1 -> x0, waiting for transfers between devices: 103 us -> none  [shards(): new_centroids = lax.all_gather(fresh, 'dp', axis=0, tiled=True)]
    unnamed x1 -> x0, blocking collectives: 48.9 us -> none
    dot_general x1 -> x0, matrix products: 9.3 us -> none  [shards(): jnp.dot(onehot.astype(jnp.bfloat16), points, preferred_element_type=jnp.f...]
    unnamed x5 -> x4, local copies, waits for them, and re-layouts: 8.96 us -> 1.23 us
    mul x0 -> x1, other arithmetic: none -> 3.78 us  [shards(): pair.astype(jnp.float32) * scale]
    dot_general x1, matrix products: 5.07 us -> 8.53 us  [shards(): lax.dot_general(points, piece, (((1,), (1,)), ((), ())), preferred_elemen...]
  transfers between devices with their start and end apart: 3 -> 1, of which waited for: 2 -> 0; matrix products, arithmetic and copies ran while one was open for 4% -> 4% of each run, Pallas kernels for 0% -> 81%
where the time goes in v1:
time: 193 us
  Pallas kernels  156 us (81%)
  between operations  14.1 us (7%)
  other arithmetic  11.6 us (6%)
  matrix products  8.53 us (4%)
  local copies, waits for them, and re-layouts  2.2 us (1%)
    pallas_call x1, Pallas kernels, shards(): pl.pallas_call(functools.partial(update_kernel, z_n, shard_rows), out_sha...  156 us
    dot_general x1, matrix products, shards(): lax.dot_general(points, piece, (((1,), (1,)), ((), ())), preferred_elemen...  8.53 us
    reduce_sum x1, other arithmetic, shards(): cent_sq = jnp.sum(piece_f * piece_f, axis=1)  5.17 us
  transfers between devices with their start and end apart: 1, of which 0 were waited for; matrix products, arithmetic and copies ran while one was open for 4% of the time, Pallas kernels for 81%

profile of v1, /device:TPU:0, one launch (start us, length us, event | category | flops | bytes accessed | tf_op | source)
XLA Modules:
  0.0 193.1 jit_solution(2933502835144660755)
XLA Ops:
  7.2 0.0 all-gather.2.cloned.1.call-start
  7.2 0.7 all-gather.2.cloned.1.call-update
  7.9 1.0 constant_dynamic-slice_fusion.prior_ref
  8.9 0.7 compare_select_fusion
  9.6 0.0 copy-start
  9.6 1.2 copy-done
  10.8 155.9 %shard_map.59 = s32[16,136,512]{2,1,0:T(8,128)S(1)} custom-call(bf16[512,1024]{1,0:T(8,128)(2,1)S(1)} %copy-done, s32[8,512]{1,0:T(8,128)S(1)} %broadcast_in_dim.7.id_ref, bf16[128,1024]{1,0:T(8,128)(2,1)S(1)} %constant_dynamic-slice_fusion.prior_ref), custom_call_target="tpu_custom_call" | custom-call | bytes 209715200 | tf_op jit(solution)/shard_map/pallas_call | solution.py:189
  166.8 0.3 multiply_reduce_fusion.1
  167.1 1.1 slice_shift-right-arithmetic_fusion
  168.1 3.8 %fusion = f32[2048,1024]{1,0:T(8,128)} fusion(s32[2048,512]{1,0:T(8,128)S(1)} %bitcast.6, s32[2048,512]{1,0:T(8,128)S(1)} %bitcast.5, f32[2048]{0:T(1024)S(1)} %bitcast.7), kind=kLoop, calls=%fused_computation.2 | loop fusion | flops 6291456 | bytes 16785408 | tf_op jit(solution)/shard_map/mul | solution.py:216
  171.9 0.0 copy-start.1
  171.9 0.0 all-gather.2.cloned.1.call-done
  171.9 5.2 %multiply_reduce_fusion = f32[4096]{0:T(1024)S(1)} fusion(bf16[4096,1024]{1,0:T(8,128)(2,1)} %all-gather.2.cloned.1.call-done), kind=kLoop, calls=%fused_computation | loop fusion | flops 12578816 | bytes 8404992 | tf_op jit(solution)/shard_map/reduce_sum | solution.py:225
  177.1 0.0 copy-done.1
  177.1 8.5 %add_reduce_fusion = f32[512]{0:T(512)S(1)} fusion(bf16[512,1024]{1,0:T(8,128)(2,1)S(1)} %copy-done.1, bf16[4096,1024]{1,0:T(8,128)(2,1)} %all-gather.2.cloned.1.call-done, f32[4096]{0:T(1024)S(1)} %multiply_reduce_fusion, f32[512]{0:T(512)S(1)} %multiply_reduce_fusion.1), kind=kOutput, calls=%fused_computation.3 | convolution fusion | flops 4303355392 | bytes 9457664 | tf_op jit(solution)/shard_map/dot_general | solution.py:219
  185.6 0.6 broadcast_multiply_fusion
  (2 shorter events, 0.0 us)
Async XLA Ops:
  7.2 164.7 %all-gather.2.cloned.1.call-start = ((), (), s32[]{:S(2)}) async-start(), calls=%async_computation | async-start | bytes 12582912 | tf_op jit(solution)/shard_map/all_gather | solution.py:218
  9.6 1.2 copy-start
  171.9 5.2 %copy-start.1 = (bf16[512,1024]{1,0:T(8,128)(2,1)S(1)}, bf16[512,1024]{1,0:T(8,128)(2,1)}, u32[]{:S(2)}) copy-start(bf16[512,1024]{1,0:T(8,128)(2,1)} %p_ref.1) | copy-start | bytes 3145732
Sparse Core Ops, SparseCore 0:
  9.5 22.5 all-gather.1

commit v2 on v0

v2 whole, which is shorter than its diff:
```python
import functools

import jax
import jax.numpy as jnp
from jax import lax
from jax.experimental import pallas as pl
from jax.experimental.pallas import tpu as pltpu
from jax.sharding import Mesh
from jax.sharding import PartitionSpec as P

STEPS = 32000.0
TINY = 2.0**-100
EXTRA = 8
PLANE = 4
LANES = 128
CHUNKS = 2
MESH = pl.DeviceIdType.MESH


def remote(src, dst, send, recv, device):
    return pltpu.make_async_remote_copy(
        src_ref=src, dst_ref=dst, send_sem=send, recv_sem=recv, device_id=device, device_id_type=MESH
    )


def update_kernel(
    z_n, shard_rows, p_ref, id_ref, prior_ref, c_ref, out_ref, low_ref,
    crecv, near, idn, acc, mrecv, red, zright, zleft,
    cs, cr, ids_s, ids_r, ps, pr, ms, mr, rs, rr, ls, lr,
    grs, grr, gls, glr, xs, xr, ys, yr, ds_, dr,
):
    z, q, m = lax.axis_index("z"), lax.axis_index("q"), lax.axis_index("mp")
    nx = q + 1 - 2 * lax.rem(q, 2)
    ny = lax.rem(q + 2, PLANE)
    nd = ny + 1 - 2 * lax.rem(ny, 2)
    other = 1 - m
    rows, width = p_ref.shape
    block = prior_ref.shape[0]
    half = rows // 2
    part = width // CHUNKS
    code_w = part // 2
    last = z_n - 1
    up, down = lax.rem(z + 1, z_n), lax.rem(z + last, z_n)

    barrier = pltpu.get_barrier_semaphore()
    peers = [(z, nx, m), (z, ny, m), (z, nd, m), (z, q, other), (up, q, m), (down, q, m)]
    for peer in peers:
        pl.semaphore_signal(barrier, inc=1, device_id=peer, device_id_type=MESH)
    pl.semaphore_wait(barrier, len(peers))

    id_copies = [
        remote(id_ref, idn.at[k], ids_s.at[k], ids_r.at[k], (z, to, m))
        for k, to in enumerate((nx, ny, nd))
    ]
    lo, hi = pl.ds(0, half), pl.ds(half, half)

    def gather_copies(c):
        cols = pl.ds(c * part, part)

        def piece(k, src, slot, span, to):
            return remote(src, near.at[c, slot, span], ps.at[c, k], pr.at[c, k], (z, to, m))

        return (
            piece(0, p_ref.at[lo, cols], 0, lo, nx),
            piece(1, p_ref.at[hi, cols], 1, hi, ny),
            piece(2, p_ref.at[hi, cols], 0, hi, nx),
            piece(3, p_ref.at[lo, cols], 1, lo, ny),
            piece(4, near.at[c, 0, lo], 2, lo, ny),
            piece(5, near.at[c, 1, hi], 2, hi, nx),
        )

    gathers = [gather_copies(c) for c in range(CHUNKS)]

    def width_of(c):
        return part + (LANES if c == 0 else 0)

    def add(c, ids, pts, first):
        def tile(t, carry):
            base = (t // z_n) * shard_rows + (lax.rem(t, z_n) * PLANE + q) * block
            row = base + lax.broadcasted_iota(jnp.int32, (block, rows), 0)
            hit = jnp.where(row == ids[0:1, :], 1.0, 0.0)
            s = jnp.dot(hit.astype(jnp.bfloat16), pts[...], preferred_element_type=jnp.float32)
            if first:
                acc[c, t, :, :part] = s
            else:
                acc[c, t, :, :part] += s
            if c == 0:
                count = jnp.broadcast_to(jnp.sum(hit, axis=1, keepdims=True), (block, LANES))
                if first:
                    acc[c, t, :, part:] = count
                else:
                    acc[c, t, :, part:] += count
            return carry

        lax.fori_loop(0, 2 * z_n, tile, 0)

    ctile = 256

    def lowest(cents, first):
        def tile(t, best):
            tile_ref = cents[pl.ds(pl.multiple_of(t * ctile, ctile), ctile), :]
            wide = tile_ref.astype(jnp.float32)
            sq = jnp.sum(wide * wide, axis=1, keepdims=True)
            inner = lax.dot_general(
                tile_ref, p_ref[...], (((1,), (1,)), ((), ())), preferred_element_type=jnp.float32
            )
            return jnp.minimum(best, jnp.min(sq - 2.0 * inner, axis=0, keepdims=True))

        start = jnp.full((1, rows), jnp.inf, jnp.float32) if first else low_ref[0:1, :]
        best = lax.fori_loop(0, shard_rows // ctile, tile, start)
        low_ref[...] = jnp.broadcast_to(best, low_ref.shape)

    ccopy = remote(c_ref, crecv, cs, cr, (z, q, other))
    for copy in id_copies + list(gathers[0][:4]):
        copy.start()
    ccopy.start()

    mcopies = []
    for c in range(CHUNKS):
        a, b2, b, d, e, f = gathers[c]
        add(c, id_ref, p_ref.at[:, pl.ds(c * part, part)], True)
        a.wait_recv()
        e.start()
        b2.wait_recv()
        f.start()
        if c + 1 < CHUNKS:
            for copy in gathers[c + 1][:4]:
                copy.start()
        if c == 0:
            lowest(c_ref, True)
            for copy in id_copies:
                copy.wait_recv()
        b.wait_recv()
        add(c, idn.at[0], near.at[c, 0], False)
        d.wait_recv()
        add(c, idn.at[1], near.at[c, 1], False)
        if c == CHUNKS - 1:
            ccopy.wait_recv()
            lowest(crecv, False)
        e.wait_recv()
        f.wait_recv()
        add(c, idn.at[2], near.at[c, 2], False)
        w = pl.ds(0, width_of(c))
        copy = remote(
            acc.at[c, pl.ds(other * z_n, z_n), :, w], mrecv.at[c, :, :, w],
            ms.at[c], mr.at[c], (z, q, other),
        )
        copy.start()
        mcopies.append(copy)

    def right(c, t):
        w = pl.ds(0, width_of(c))
        return remote(
            red.at[c, t, :, w], zright.at[c, t, :, w], rs.at[c, t], rr.at[c, t], (up, q, m)
        )

    def left(c, t):
        w = pl.ds(0, width_of(c))
        return remote(
            red.at[c, t, :, w], zleft.at[c, t, :, w], ls.at[c, t], lr.at[c, t], (down, q, m)
        )

    for c in range(CHUNKS):
        mcopies[c].wait_recv()
        w = width_of(c)
        for t in range(z_n):
            red[c, t, :, :w] = acc[c, m * z_n + t, :, :w] + mrecv[c, t, :, :w]

    for s in range(last):
        for c in range(CHUNKS):
            w = width_of(c)
            for far, go, land, send, more in (
                (last - s, z < last - s, zright, right, z > 0),
                (s, z > s, zleft, left, z < last),
            ):

                @pl.when(go)
                def _(c=c, w=w, far=far, land=land, send=send, more=more):
                    @pl.when(more)
                    def _():
                        send(c, far).wait_recv()
                        red[c, far, :, :w] += land[c, far, :, :w]

                    send(c, far).start()

    own = z * PLANE + q

    def xcopy(c, n, to_q):
        at = out_ref.at[c, n * PLANE + to_q]
        return remote(at, at, xs.at[c, n], xr.at[c, n], (z, nx, m))

    def ycopy(c, n, to_q):
        at = out_ref.at[c, n * PLANE + to_q]
        return remote(at, at, ys.at[c, n], yr.at[c, n], (z, ny, m))

    def dcopy(c, n, by_x):
        at = out_ref.at[c, n * PLANE + (nx if by_x else ny)]
        return remote(at, at, ds_.at[c, n], dr.at[c, n], (z, ny if by_x else nx, m))

    def gright(c, n):
        at = out_ref.at[c, n * PLANE + q]
        return remote(at, at, grs.at[c, n], grr.at[c, n], (up, q, m))

    def gleft(c, n):
        at = out_ref.at[c, n * PLANE + q]
        return remote(at, at, gls.at[c, n], glr.at[c, n], (down, q, m))

    count = None
    for c in range(CHUNKS):
        w = width_of(c)

        @pl.when(z > 0)
        def _(c=c, w=w):
            right(c, z).wait_recv()
            red[c, z, :, :w] += zright[c, z, :, :w]

        @pl.when(z < last)
        def _(c=c, w=w):
            left(c, z).wait_recv()
            red[c, z, :, :w] += zleft[c, z, :, :w]

        if c == 0:
            count = red[c, z, :, part : part + 1]
        prior = prior_ref[:, c * part : (c + 1) * part].astype(jnp.float32)
        fresh = jnp.where(count > 0.5, red[c, z, :, :part] / jnp.maximum(count, 1.0), prior)
        top = jnp.max(jnp.abs(fresh), axis=1, keepdims=True)
        power = jnp.ceil(jnp.log2(jnp.maximum(top, TINY)))
        code = jnp.floor(fresh * jnp.exp2(-power) * STEPS + 0.5).astype(jnp.int32)
        out_ref[c, own, :block] = (code[:, :code_w] << 16) | (code[:, code_w:] & 0xFFFF)
        at_row = lax.broadcasted_iota(jnp.int32, (block, LANES), 0)
        at_lane = lax.broadcasted_iota(jnp.int32, (block, LANES), 1)
        flat = jnp.sum(jnp.where(at_row == at_lane, power, 0.0), axis=0, keepdims=True)
        out_ref[c, own, block:] = jnp.zeros((EXTRA, code_w), jnp.int32)
        out_ref[c, own, block:, :LANES] = jnp.broadcast_to(flat.astype(jnp.int32), (EXTRA, LANES))

        @pl.when(z < last)
        def _(c=c):
            gright(c, z).start()

        @pl.when(z > 0)
        def _(c=c):
            gleft(c, z).start()

        xcopy(c, z, q).start()
        ycopy(c, z, q).start()

    def relay(c, n, by_x):
        if by_x:
            xcopy(c, n, nx).wait_recv()
        else:
            ycopy(c, n, ny).wait_recv()
        dcopy(c, n, by_x).start()

    def settle(c, n, by_x):
        if by_x:
            ycopy(c, n, ny).wait_recv()
        else:
            xcopy(c, n, nx).wait_recv()
        dcopy(c, n, by_x).wait_recv()

    def each(k, c, action):
        if k == 0:
            action(c, z, c % 2 == 0)
            return

        @pl.when(z >= k)
        def _():
            action(c, z - k, k % 2 == 0)

        @pl.when(z + k <= last)
        def _():
            action(c, z + k, k % 2 == 1)

    for k in range(z_n):
        for c in range(CHUNKS):
            if k > 0:

                @pl.when(z >= k)
                def _(c=c, k=k):
                    gright(c, z - k).wait_recv()

                    @pl.when(z < last)
                    def _():
                        gright(c, z - k).start()

                    xcopy(c, z - k, q).start()
                    ycopy(c, z - k, q).start()

                @pl.when(z + k <= last)
                def _(c=c, k=k):
                    gleft(c, z + k).wait_recv()

                    @pl.when(z > 0)
                    def _():
                        gleft(c, z + k).start()

                    xcopy(c, z + k, q).start()
                    ycopy(c, z + k, q).start()

        if k > 0:
            for c in range(CHUNKS):
                each(k - 1, c, relay)
    for c in range(CHUNKS):
        each(last, c, relay)
    for k in range(z_n):
        for c in range(CHUNKS):
            each(k, c, settle)

    for copy in id_copies + [ccopy] + mcopies:
        copy.wait_send()
    for c in range(CHUNKS):
        for copy in gathers[c]:
            copy.wait_send()
        for t in range(z_n):

            @pl.when(z < t)
            def _(c=c, t=t):
                right(c, t).wait_send()

            @pl.when(z > t)
            def _(c=c, t=t):
                left(c, t).wait_send()

            @pl.when((z >= t) & (z < last))
            def _(c=c, t=t):
                gright(c, t).wait_send()

            @pl.when((z <= t) & (z > 0))
            def _(c=c, t=t):
                gleft(c, t).wait_send()

            xcopy(c, t, q).wait_send()
            ycopy(c, t, q).wait_send()
            dcopy(c, t, True).wait_send()


def shards(points, centroids, assign, keep_mask):
    rows, width = points.shape
    shard_rows = centroids.shape[0]
    z_n = lax.axis_size("z")
    dp_n = z_n * PLANE
    block = shard_rows // dp_n
    own = lax.axis_index("z") * PLANE + lax.axis_index("q")
    ids = jnp.where(keep_mask > 0, assign, -1)
    ids = jnp.broadcast_to(ids[None, :], (8, rows))
    prior = lax.dynamic_slice_in_dim(centroids, own * block, block, 0)
    vmem = pl.BlockSpec(memory_space=pltpu.VMEM)
    dma = pltpu.SemaphoreType.DMA
    part = width // CHUNKS
    wide = part + LANES
    per = dma((CHUNKS, z_n))
    back, low = pl.pallas_call(
        functools.partial(update_kernel, z_n, shard_rows),
        out_shape=(
            jax.ShapeDtypeStruct((CHUNKS, dp_n, block + EXTRA, part // 2), jnp.int32),
            jax.ShapeDtypeStruct((8, rows), jnp.float32),
        ),
        in_specs=[vmem] * 4,
        out_specs=(vmem, vmem),
        scratch_shapes=[
            pltpu.VMEM((shard_rows, width), centroids.dtype),
            pltpu.VMEM((CHUNKS, 3, rows, part), points.dtype),
            pltpu.VMEM((3, 8, rows), jnp.int32),
            pltpu.VMEM((CHUNKS, 2 * z_n, block, wide), jnp.float32),
            pltpu.VMEM((CHUNKS, z_n, block, wide), jnp.float32),
            pltpu.VMEM((CHUNKS, z_n, block, wide), jnp.float32),
            pltpu.VMEM((CHUNKS, z_n, block, wide), jnp.float32),
            pltpu.VMEM((CHUNKS, z_n, block, wide), jnp.float32),
            dma, dma, dma((3,)), dma((3,)), dma((CHUNKS, 6)), dma((CHUNKS, 6)),
            dma((CHUNKS,)), dma((CHUNKS,)),
            per, per, per, per, per, per, per, per, per, per, per, per, per, per,
        ],
        compiler_params=pltpu.CompilerParams(
            collective_id=0, has_side_effects=True, vmem_limit_bytes=56 * 1024 * 1024
        ),
        cost_estimate=pl.CostEstimate(
            flops=0, bytes_accessed=200 * 1024 * 1024, transcendentals=0
        ),
    )(points, ids, prior, centroids)
    codes = back[:, :, :block]
    powers = back[:, :, block, :block].astype(jnp.float32)
    scale = (jnp.exp2(powers) / STEPS)[:, :, :, None]
    pieces = []
    for c in range(CHUNKS):
        pieces += [(codes[c] >> 16) * scale[c], ((codes[c] << 16) >> 16) * scale[c]]
    new_centroids = jnp.concatenate(pieces, axis=2).reshape(shard_rows, width)
    point_f = points.astype(jnp.float32)
    point_sq = jnp.sum(point_f * point_f, axis=1)
    return new_centroids, (point_sq + low[0]) / width


def solution(mesh):
    dp, mp = mesh.shape["dp"], mesh.shape["mp"]
    grid = Mesh(mesh.devices.reshape(dp // PLANE, PLANE, mp), ("z", "q", "mp"))
    rows = ("z", "q", "mp")
    in_specs = (P(rows, None), P("mp", None), P(rows), P(rows))
    out_specs = (P("mp", None), P(rows))
    return jax.shard_map(shards, mesh=grid, in_specs=in_specs, out_specs=out_specs, check_vma=False)
```

time: 339 us -> 154 us (0.45)
  the two profiles are of different devices: /device:TPU:0 before, /device:TPU:17 now
where the time goes in v2:
time: 154 us
  Pallas kernels  138 us (90%)
  other arithmetic  12.4 us (8%)
  local copies, waits for them, and re-layouts  2.99 us (2%)
    pallas_call x1, Pallas kernels, shards(): pl.pallas_call(functools.partial(update_kernel, z_n, shard_rows), out_sha...  138 us
    concatenate x1, other arithmetic, shards(): new_centroids = jnp.concatenate(pieces, axis=2).reshape(shard_rows, width)  4.06 us
    convert_element_type x1, other arithmetic, shards(): pieces += [(codes[c] >> 16) * scale[c], (codes[c] << 16 >> 16) * scale[c]]  3.37 us

profile of v2, /device:TPU:17, one launch (start us, length us, event | category | flops | bytes accessed | tf_op | source)
XLA Modules:
  0.0 154.2 jit_solution(5380713116310855407)
XLA Ops:
  0.6 0.7 compare_select_fusion
  1.3 1.5 multiply_reduce_fusion
  2.8 0.6 broadcast_in_dim.12.id_ref
  3.4 1.7 %constant_dynamic-slice_fusion.prior_ref = bf16[128,1024]{1,0:T(8,128)(2,1)} fusion(bf16[2048,1024]{1,0:T(8,128)(2,1)} %c_ref.1, s32[]{:T(128)S(6)} %select_n.8), kind=kLoop, calls=%fused_computation.13 | loop fusion | bytes 524292 | tf_op jit(solution)/shard_map/dynamic_slice | solution.py:346
  5.1 138.1 %shard_map.59 = (s32[2,16,136,256]{3,2,1,0:T(8,128)}, f32[8,512]{1,0:T(8,128)}) custom-call(bf16[512,1024]{1,0:T(8,128)(2,1)} %p_ref.1, s32[8,512]{1,0:T(8,128)} %broadcast_in_dim.12.id_ref, bf16[128,1024]{1,0:T(8,128)(2,1)} %constant_dynamic-slice_fusion.prior_ref, bf16[2048,1024]{1,0:T(8,128)(2,1)} %c_ref.1), custom_call_target="tpu_custom_call" | custom-call | bytes 209715200 | tf_op jit(solution)/shard_map/pallas_call | solution.py:352
  143.2 0.7 slice.34
  143.9 0.6 add_multiply_fusion
  144.5 0.9 exponential_multiply_fusion
  145.5 3.4 %shift-right-arithmetic_convert_fusion.3 = (f32[1,16,128,256]{3,2,1,0:T(8,128)S(1)}, f32[1,16,128,256]{3,2,1,0:T(8,128)S(1)}, f32[1,16,128,256]{3,2,1,0:T(8,128)S(1)}, f32[1,16,128,256]{3,2,1,0:T(8,128)S(1)}) fusion(s32[2,16,136,256]{3,2,1,0:T(8,128)} %get-tuple-element.4), kind=kLoop, calls=%fused_computation.9 | loop fusion | flops 5242880 | bytes 12582912 | tf_op jit(solution)/shard_map/convert_element_type | solution.py:385
  148.8 1.3 bitcast_multiply_fusion.1
  150.1 4.1 %pad_maximum_fusion = f32[2048,1024]{1,0:T(8,128)} fusion(f32[2048,256]{1,0:T(8,128)S(1)} %get-tuple-element.15, f32[2048,256]{1,0:T(8,128)S(1)} %get-tuple-element.14, f32[2048,256]{1,0:T(8,128)S(1)} %get-tuple-element.16, f32[2048,256]{1,0:T(8,128)S(1)} %get-tuple-element.17), kind=kLoop, calls=%fused_computation | loop fusion | flops 6291456 | bytes 16777216 | tf_op jit(solution)/shard_map/concatenate | solution.py:386
  (1 shorter events, 0.0 us)

commit v3 on v2

--- a/solution.py
+++ b/solution.py
@@ -25,8 +25,8 @@
 
 def update_kernel(
     z_n, shard_rows, p_ref, id_ref, prior_ref, c_ref, out_ref, low_ref,
-    crecv, near, idn, acc, mrecv, red, zright, zleft,
-    cs, cr, ids_s, ids_r, ps, pr, ms, mr, rs, rr, ls, lr,
+    crecv, near, idn, acc, mrecv, red, zright,
+    cs, cr, ids_s, ids_r, ps, pr, ms, mr, rs, rr,
     grs, grr, gls, glr, xs, xr, ys, yr, ds_, dr,
 ):
     z, q, m = lax.axis_index("z"), lax.axis_index("q"), lax.axis_index("mp")
@@ -43,7 +43,8 @@
     up, down = lax.rem(z + 1, z_n), lax.rem(z + last, z_n)
 
     barrier = pltpu.get_barrier_semaphore()
-    peers = [(z, nx, m), (z, ny, m), (z, nd, m), (z, q, other), (up, q, m), (down, q, m)]
+    peers = [(z, nx, m), (z, ny, m), (z, nd, m), (z, q, other)]
+    peers += [(lax.rem(z + k, z_n), q, m) for k in range(1, z_n)]
     for peer in peers:
         pl.semaphore_signal(barrier, inc=1, device_id=peer, device_id_type=MESH)
     pl.semaphore_wait(barrier, len(peers))
@@ -116,8 +117,9 @@
     ccopy.start()
 
     mcopies = []
-    for c in range(CHUNKS):
-        a, b2, b, d, e, f = gathers[c]
+
+    def open_gather(c):
+        a, b2, _, _, e, f = gathers[c]
         add(c, id_ref, p_ref.at[:, pl.ds(c * part, part)], True)
         a.wait_recv()
         e.start()
@@ -126,6 +128,9 @@
         if c + 1 < CHUNKS:
             for copy in gathers[c + 1][:4]:
                 copy.start()
+
+    def close_gather(c):
+        _, _, b, d, e, f = gathers[c]
         if c == 0:
             lowest(c_ref, True)
             for copy in id_copies:
@@ -134,7 +139,7 @@
         add(c, idn.at[0], near.at[c, 0], False)
         d.wait_recv()
         add(c, idn.at[1], near.at[c, 1], False)
-        if c == CHUNKS - 1:
+        if c == 0:
             ccopy.wait_recv()
             lowest(crecv, False)
         e.wait_recv()
@@ -148,40 +153,21 @@
         copy.start()
         mcopies.append(copy)
 
-    def right(c, t):
+    def direct(c, k):
         w = pl.ds(0, width_of(c))
+        to = lax.rem(z + k, z_n)
         return remote(
-            red.at[c, t, :, w], zright.at[c, t, :, w], rs.at[c, t], rr.at[c, t], (up, q, m)
+            red.at[c, to, :, w], zright.at[c, k, :, w], rs.at[c, k], rr.at[c, k], (to, q, m)
         )
 
-    def left(c, t):
-        w = pl.ds(0, width_of(c))
-        return remote(
-            red.at[c, t, :, w], zleft.at[c, t, :, w], ls.at[c, t], lr.at[c, t], (down, q, m)
-        )
-
-    for c in range(CHUNKS):
+    def combine(c):
         mcopies[c].wait_recv()
         w = width_of(c)
-        for t in range(z_n):
+        for k in range(1, z_n + 1):
+            t = lax.rem(z + k, z_n)
             red[c, t, :, :w] = acc[c, m * z_n + t, :, :w] + mrecv[c, t, :, :w]
-
-    for s in range(last):
-        for c in range(CHUNKS):
-            w = width_of(c)
-            for far, go, land, send, more in (
-                (last - s, z < last - s, zright, right, z > 0),
-                (s, z > s, zleft, left, z < last),
-            ):
-
-                @pl.when(go)
-                def _(c=c, w=w, far=far, land=land, send=send, more=more):
-                    @pl.when(more)
-                    def _():
-                        send(c, far).wait_recv()
-                        red[c, far, :, :w] += land[c, far, :, :w]
-
-                    send(c, far).start()
+            if k < z_n:
+                direct(c, k).start()
 
     own = z * PLANE + q
 
@@ -205,19 +191,12 @@
         at = out_ref.at[c, n * PLANE + q]
         return remote(at, at, gls.at[c, n], glr.at[c, n], (down, q, m))
 
-    count = None
-    for c in range(CHUNKS):
+    def publish(c, count):
         w = width_of(c)
 
-        @pl.when(z > 0)
-        def _(c=c, w=w):
-            right(c, z).wait_recv()
-            red[c, z, :, :w] += zright[c, z, :, :w]
-
-        @pl.when(z < last)
-        def _(c=c, w=w):
-            left(c, z).wait_recv()
-            red[c, z, :, :w] += zleft[c, z, :, :w]
+        for k in range(1, z_n):
+            direct(c, k).wait_recv()
+            red[c, z, :, :w] += zright[c, k, :, :w]
 
         if c == 0:
             count = red[c, z, :, part : part + 1]
@@ -243,6 +222,7 @@
 
         xcopy(c, z, q).start()
         ycopy(c, z, q).start()
+        return count
 
     def relay(c, n, by_x):
         if by_x:
@@ -271,35 +251,45 @@
         def _():
             action(c, z + k, k % 2 == 1)
 
-    for k in range(z_n):
+    def spread(c, k):
+        @pl.when(z >= k)
+        def _():
+            gright(c, z - k).wait_recv()
+
+            @pl.when(z < last)
+            def _():
+                gright(c, z - k).start()
+
+            xcopy(c, z - k, q).start()
+            ycopy(c, z - k, q).start()
+
+        @pl.when(z + k <= last)
+        def _():
+            gleft(c, z + k).wait_recv()
+
+            @pl.when(z > 0)
+            def _():
+                gleft(c, z + k).start()
+
+            xcopy(c, z + k, q).start()
+            ycopy(c, z + k, q).start()
+
+        each(k - 1, c, relay)
+
+    open_gather(0)
+    close_gather(0)
+    for c in range(CHUNKS):
+        if c + 1 < CHUNKS:
+            open_gather(c + 1)
+        combine(c)
+        if c + 1 < CHUNKS:
+            close_gather(c + 1)
+    count = None
+    for c in range(CHUNKS):
+        count = publish(c, count)
+    for k in range(1, z_n):
         for c in range(CHUNKS):
-            if k > 0:
-
-                @pl.when(z >= k)
-                def _(c=c, k=k):
-                    gright(c, z - k).wait_recv()
-
-                    @pl.when(z < last)
-                    def _():
-                        gright(c, z - k).start()
-
-                    xcopy(c, z - k, q).start()
-                    ycopy(c, z - k, q).start()
-
-                @pl.when(z + k <= last)
-                def _(c=c, k=k):
-                    gleft(c, z + k).wait_recv()
-
-                    @pl.when(z > 0)
-                    def _():
-                        gleft(c, z + k).start()
-
-                    xcopy(c, z + k, q).start()
-                    ycopy(c, z + k, q).start()
-
-        if k > 0:
-            for c in range(CHUNKS):
-                each(k - 1, c, relay)
+            spread(c, k)
     for c in range(CHUNKS):
         each(last, c, relay)
     for k in range(z_n):
@@ -313,13 +303,8 @@
             copy.wait_send()
         for t in range(z_n):
 
-            @pl.when(z < t)
-            def _(c=c, t=t):
-                right(c, t).wait_send()
-
-            @pl.when(z > t)
-            def _(c=c, t=t):
-                left(c, t).wait_send()
+            if t > 0:
+                direct(c, t).wait_send()
 
             @pl.when((z >= t) & (z < last))
             def _(c=c, t=t):
@@ -365,10 +350,9 @@
             pltpu.VMEM((CHUNKS, z_n, block, wide), jnp.float32),
             pltpu.VMEM((CHUNKS, z_n, block, wide), jnp.float32),
             pltpu.VMEM((CHUNKS, z_n, block, wide), jnp.float32),
-            pltpu.VMEM((CHUNKS, z_n, block, wide), jnp.float32),
             dma, dma, dma((3,)), dma((3,)), dma((CHUNKS, 6)), dma((CHUNKS, 6)),
             dma((CHUNKS,)), dma((CHUNKS,)),
-            per, per, per, per, per, per, per, per, per, per, per, per, per, per,
+            per, per, per, per, per, per, per, per, per, per, per, per,
         ],
         compiler_params=pltpu.CompilerParams(
             collective_id=0, has_side_effects=True, vmem_limit_bytes=56 * 1024 * 1024

time: 154 us -> 143 us (0.929)
  the two profiles are of different devices: /device:TPU:17 before, /device:TPU:0 now
where the time goes in v3:
time: 143 us; the launch traced here: 141 us
  Pallas kernels  125 us (87%)
  other arithmetic  12.4 us (9%)
  local copies, waits for them, and re-layouts  2.99 us (2%)
    pallas_call x1, Pallas kernels, shards(): pl.pallas_call(functools.partial(update_kernel, z_n, shard_rows), out_sha...  125 us
    concatenate x1, other arithmetic, shards(): new_centroids = jnp.concatenate(pieces, axis=2).reshape(shard_rows, width)  4.06 us
    convert_element_type x1, other arithmetic, shards(): pieces += [(codes[c] >> 16) * scale[c], (codes[c] << 16 >> 16) * scale[c]]  3.37 us

profile of v3, /device:TPU:0, one launch (start us, length us, event | category | flops | bytes accessed | tf_op | source)
XLA Modules:
  0.0 140.8 jit_solution(10201832552461841946)
XLA Ops:
  0.6 0.7 compare_select_fusion
  1.3 1.5 %multiply_reduce_fusion = f32[512]{0:T(512)S(1)} fusion(bf16[512,1024]{1,0:T(8,128)(2,1)} %p_ref.1), kind=kLoop, calls=%fused_computation.5 | loop fusion | flops 1572352 | bytes 1050624 | tf_op jit(solution)/shard_map/reduce_sum | solution.py:372
  2.8 0.6 broadcast_in_dim.12.id_ref
  3.4 1.7 %constant_dynamic-slice_fusion.prior_ref = bf16[128,1024]{1,0:T(8,128)(2,1)} fusion(bf16[2048,1024]{1,0:T(8,128)(2,1)} %c_ref.1, s32[]{:T(128)S(6)} %select_n.8), kind=kLoop, calls=%fused_computation.13 | loop fusion | bytes 524292 | tf_op jit(solution)/shard_map/dynamic_slice | solution.py:331
  5.1 124.7 %shard_map.59 = (s32[2,16,136,256]{3,2,1,0:T(8,128)}, f32[8,512]{1,0:T(8,128)}) custom-call(bf16[512,1024]{1,0:T(8,128)(2,1)} %p_ref.1, s32[8,512]{1,0:T(8,128)} %broadcast_in_dim.12.id_ref, bf16[128,1024]{1,0:T(8,128)(2,1)} %constant_dynamic-slice_fusion.prior_ref, bf16[2048,1024]{1,0:T(8,128)(2,1)} %c_ref.1), custom_call_target="tpu_custom_call" | custom-call | bytes 209715200 | tf_op jit(solution)/shard_map/pallas_call | solution.py:337
  129.9 0.7 slice.34
  130.6 0.6 add_multiply_fusion
  131.2 0.9 exponential_multiply_fusion
  132.1 3.4 %shift-right-arithmetic_convert_fusion.3 = (f32[1,16,128,256]{3,2,1,0:T(8,128)S(1)}, f32[1,16,128,256]{3,2,1,0:T(8,128)S(1)}, f32[1,16,128,256]{3,2,1,0:T(8,128)S(1)}, f32[1,16,128,256]{3,2,1,0:T(8,128)S(1)}) fusion(s32[2,16,136,256]{3,2,1,0:T(8,128)} %get-tuple-element.4), kind=kLoop, calls=%fused_computation.9 | loop fusion | flops 5242880 | bytes 12582912 | tf_op jit(solution)/shard_map/convert_element_type | solution.py:369
  135.5 1.3 bitcast_multiply_fusion.1
  136.8 4.1 %pad_maximum_fusion = f32[2048,1024]{1,0:T(8,128)} fusion(f32[2048,256]{1,0:T(8,128)S(1)} %get-tuple-element.15, f32[2048,256]{1,0:T(8,128)S(1)} %get-tuple-element.14, f32[2048,256]{1,0:T(8,128)S(1)} %get-tuple-element.16, f32[2048,256]{1,0:T(8,128)S(1)} %get-tuple-element.17), kind=kLoop, calls=%fused_computation | loop fusion | flops 6291456 | bytes 16777216 | tf_op jit(solution)/shard_map/concatenate | solution.py:370
  (1 shorter events, 0.0 us)
